TPU v7x, 16 devices: a whole 2x2x2 slice. The times are simulated.
16 devices in a mesh: data: 4 (over z, y), seq: 4 (over x, core).
Axes of the slice: x: 2, y: 2, z: 2, core: 2. Of those that a mesh axis runs over, the one named last changes fastest.
Arguments:
- x: bfloat16 [8192, 4096], P(('data', 'seq')), parts along dimension 0
- g1: float32 [4096], replicated
- b1: float32 [4096], replicated
- g2: float32 [4096], replicated
- b2: float32 [4096], replicated
- wqkv: bfloat16 [4096, 12288], replicated
- wo: bfloat16 [32, 128, 4096], replicated
- w1: bfloat16 [4096, 16384], replicated
- w2: bfloat16 [16384, 4096], replicated
Outputs:
- output: bfloat16 [8192, 4096], P(('data', 'seq')), parts along dimension 0
There are 4 independent parts. A program takes and returns all parts, laid end to end along the dimension named above; an argument that names none is the same for every part.
All inputs are finite; a program needn't handle non-finite values.
Results may differ from a plain program's by a relative error of at most 0.00239018.
Values are sent between devices in bfloat16 or wider.
A program may use at most 1.75 GiB of HBM per device.

v0:
```python
import functools

import jax
import jax.numpy as jnp
from jax import lax
from jax.experimental import pallas as pl
from jax.experimental.pallas import tpu as pltpu
from jax.sharding import PartitionSpec as P

EPS = 1e-5
NEG = -1e30
F32 = jnp.float32
BF16 = jnp.bfloat16
VMEM = 60 * 1024 * 1024


def _cost(flops, nbytes):
    return pl.CostEstimate(flops=int(flops), bytes_accessed=int(nbytes), transcendentals=0)


def _dot(a, b):
    return jnp.dot(a, b, preferred_element_type=F32)


MESH = pl.DeviceIdType.MESH
LO = 64


def _rope_tables(s, dh):
    half = dh // 2
    e = lax.broadcasted_iota(jnp.int32, (1, dh), 1)
    inv = 10000.0 ** (-2.0 * (e % half).astype(F32) / dh)
    lo = jnp.arange(LO).astype(F32)[:, None] * inv
    hi = (LO * jnp.arange(s // LO)).astype(F32)[:, None] * inv
    return jnp.cos(lo), jnp.sin(lo), jnp.cos(hi), jnp.sin(hi)


def _front(x, g1, b1, g2, b2, tabs, wqkv, w1):
    r, d = x.shape
    f = w1.shape[1]
    w3 = wqkv.shape[1] // 3
    hw = w3 // 4
    dh = tabs[0].shape[1]
    nt = 512
    mt = 2 * nt
    cw = 256
    t1 = f // mt
    nb = hw // nt
    t2 = 3 * nb
    ntile1 = f // nt
    ntiles = ntile1 + 2 * t2
    ring = 5
    xc = 128
    steps = t1 + 2 * t2 + 1

    def body(x_ref, g1_ref, b1_ref, g2_ref, b2_ref, cl, sl, ch, sh, wqkv_ref, w1_ref,
             h_ref, qkv_ref, x_scr, rows, m_scr, w_scr, t_scr, cos_s, sin_s,
             xsem, wsem, send, recv):
        s = pl.program_id(0)
        me = lax.axis_index("seq")
        core = me % 2
        near = me + 1 - 2 * core
        far = (me + 2) % 4

        def member(k):
            return [me, near, far, 3 - me][k]

        def load(i):
            slot = i % ring

            @pl.when(i < ntile1)
            def _():
                c = pl.multiple_of(i * nt, nt)
                pltpu.make_async_copy(w1_ref.at[:, pl.ds(c, nt)], w_scr.at[slot], wsem.at[slot]).start()

            @pl.when((i >= ntile1) & (i < ntiles))
            def _():
                v = (i - ntile1) % t2
                c = pl.multiple_of((v // nb) * w3 + me * hw + (v % nb) * nt, nt)
                pltpu.make_async_copy(wqkv_ref.at[:, pl.ds(c, nt)], w_scr.at[slot], wsem.at[slot]).start()

        def ready(i):
            slot = i % ring
            pltpu.make_async_copy(w1_ref.at[:, pl.ds(0, nt)], w_scr.at[slot], wsem.at[slot]).wait()
            return slot

        def remote(src, dst, part, sem, dev):
            return pltpu.make_async_remote_copy(
                src_ref=rows.at[src, part], dst_ref=rows.at[dst, part], send_sem=send.at[sem],
                recv_sem=recv.at[sem], device_id={"seq": dev}, device_id_type=MESH)

        def to_near():
            return remote(0, 1, pl.ds(0, r), 0, near)

        def to_far(p):
            return remote(0, 2, pl.ds(p * (r // 2), r // 2), 1 + p, far)

        def onward(p):
            return remote(2, 3, pl.ds(p * (r // 2), r // 2), 3 + p, near)

        def norm(c, q, _):
            base = c * xc + q * 32
            groups = [pl.ds(pl.multiple_of(base + 16 * g, 16), 16) for g in range(2)]
            nl = d // 128

            def col(rs, j):
                return x_scr[rs, j * 128:(j + 1) * 128].astype(F32)

            def total(f):
                part = [[None] * 4 for _ in groups]
                for j in range(nl):
                    for g, rs in enumerate(groups):
                        v = f(g, col(rs, j))
                        part[g][j % 4] = v if part[g][j % 4] is None else part[g][j % 4] + v
                return [jnp.sum((p[0] + p[1]) + (p[2] + p[3]), axis=-1, keepdims=True) / d for p in part]

            mu = total(lambda g, v: v)
            var = total(lambda g, v: (v - mu[g]) * (v - mu[g]))
            rs_ = [lax.rsqrt(v + EPS) for v in var]
            for j in range(nl):
                cs = slice(j * 128, (j + 1) * 128)
                for g, rs in enumerate(groups):
                    xn = (col(rs, j) - mu[g]) * rs_[g]
                    rows[0, rs, cs] = (xn * g1_ref[:, cs] + b1_ref[:, cs]).astype(BF16)
                    m_scr[rs, cs] = (xn * g2_ref[:, cs] + b2_ref[:, cs]).astype(BF16)
            return 0

        @pl.when(s == 0)
        def _():
            def chunk(c):
                rs = pl.ds(c * xc, xc)
                return pltpu.make_async_copy(x_ref.at[rs], x_scr.at[rs], xsem.at[c])

            for c in range(r // xc):
                chunk(c).start()
            for i in range(ring):
                load(i)
            bar = pltpu.get_barrier_semaphore()
            for dev in (near, far):
                pl.semaphore_signal(bar, inc=1, device_id={"seq": dev}, device_id_type=MESH)
            for c in range(r // xc):
                chunk(c).wait()

                lax.fori_loop(0, xc // 32, functools.partial(norm, c), 0)
                if c == r // xc // 2 - 1:
                    pl.semaphore_wait(bar, 2)
                    to_far(0).start()
            to_far(1).start()
            to_near().start()
            neg = lax.broadcasted_iota(jnp.int32, (LO, dh), 1) < dh // 2
            for k in range(4):
                n = r // LO
                base = pl.ds(pl.multiple_of(member(k) * n, n), n)
                hc, hs = ch[base, :], sh[base, :]
                for i in range(n):
                    a, b = hc[i:i + 1], hs[i:i + 1]
                    sn = b * cl[...] + a * sl[...]
                    cos_s[k, i * LO:(i + 1) * LO, :] = a * cl[...] - b * sl[...]
                    sin_s[k, i * LO:(i + 1) * LO, :] = jnp.where(neg, -sn, sn)

        def gelu(cols):
            t = t_scr[:, cols]
            h_ref[:, cols] = (0.5 * t * (1.0 + lax.erf(t * (0.5 ** 0.5)))).astype(BF16)

        def mlp(first):
            slots = [ready(2 * s + half) for half in range(mt // nt)]
            for half, slot in enumerate(slots):
                for c in range(nt // cw):
                    cols = slice(half * nt + c * cw, half * nt + (c + 1) * cw)
                    if not first:
                        gelu(cols)
                    t_scr[:, cols] = _dot(m_scr[...], w_scr[slot, :, c * cw:(c + 1) * cw])
            load(2 * s + ring)
            load(2 * s + ring + 1)

        pl.when(s == 0)(lambda: mlp(True))
        pl.when((s > 0) & (s < t1))(lambda: mlp(False))

        def rope(j):
            u = s - 1 - t1
            isv = (u % t2) // nb == 2
            base = 2 * (u // t2)
            k, c = j // (nt // cw), j % (nt // cw)
            out = pl.ds(pl.multiple_of((core if k == 0 else 1 - core) * r, r), r)
            t = t_scr[:, j * cw:(j + 1) * cw].astype(BF16).astype(F32)
            for hd in range(cw // dh):
                p = t[:, hd * dh:(hd + 1) * dh]
                v = p * cos_s[base + k] + pltpu.roll(p, dh // 2, 1) * sin_s[base + k]
                lo = c * cw + hd * dh
                qkv_ref[out, lo:lo + dh] = jnp.where(isv, p, v).astype(BF16)

        def qkv(first):
            u = s - t1
            slot = ready(ntile1 + u)
            base = 2 * (u // t2)
            for j in range(mt // cw):
                cols = slice(j * cw, (j + 1) * cw)
                k, c = j // (nt // cw), j % (nt // cw)
                if first:
                    gelu(cols)
                else:
                    rope(j)
                t_scr[:, cols] = _dot(rows[base + k], w_scr[slot, :, c * cw:(c + 1) * cw])
            load(ntile1 + u + ring)

        @pl.when(s == t1)
        def _():
            to_near().wait_recv()
            to_far(0).wait_recv()
            onward(0).start()
            qkv(True)

        @pl.when(s == t1 + t2 - 2)
        def _():
            to_far(1).wait_recv()
            onward(1).start()

        @pl.when(s == t1 + t2)
        def _():
            onward(0).wait_recv()
            onward(1).wait_recv()

        pl.when((s > t1) & (s < steps - 1))(lambda: qkv(False))

        @pl.when(s == steps - 1)
        def _():
            for j in range(mt // cw):
                rope(j)

        @pl.when(s == steps - 1)
        def _():
            to_near().wait_send()
            for p in range(2):
                to_far(p).wait_send()
                onward(p).wait_send()

    def h_map(s):
        return 0, jnp.clip(s - 1, 0, t1 - 1)

    def qkv_map(s):
        u = jnp.maximum(s - 1 - t1, 0)
        chip = lax.axis_index("seq") // 2
        second = u // t2
        return chip + second * (1 - 2 * chip), u % t2

    def full(shape):
        return pl.BlockSpec(shape, lambda s: (0, 0))

    anyspace = pl.BlockSpec(memory_space=pl.ANY)
    return pl.pallas_call(
        body,
        grid=(steps,),
        in_specs=[anyspace] + [full((1, d))] * 4 + [full(t.shape) for t in tabs] + [anyspace] * 2,
        out_specs=[pl.BlockSpec((r, mt), h_map), pl.BlockSpec((2 * r, nt), qkv_map)],
        out_shape=[jax.ShapeDtypeStruct((r, f), BF16), jax.ShapeDtypeStruct((4 * r, 3 * hw), BF16)],
        scratch_shapes=[
            pltpu.VMEM((r, d), BF16), pltpu.VMEM((4, r, d), BF16), pltpu.VMEM((r, d), BF16), pltpu.VMEM((ring, d, nt), BF16),
            pltpu.VMEM((r, mt), F32), pltpu.VMEM((4, r, dh), F32), pltpu.VMEM((4, r, dh), F32),
            pltpu.SemaphoreType.DMA((r // xc,)), pltpu.SemaphoreType.DMA((ring,)),
            pltpu.SemaphoreType.DMA((5,)), pltpu.SemaphoreType.DMA((5,))],
        compiler_params=pltpu.CompilerParams(
            dimension_semantics=("arbitrary",), vmem_limit_bytes=VMEM, collective_id=0,
            has_side_effects=True),
        name="front",
        cost_estimate=_cost(2 * r * d * f + 2 * 4 * r * d * 3 * hw, 2 * d * f + 4 * d * 3 * hw),
    )(x, g1[None], b1[None], g2[None], b2[None], *tabs, wqkv, w1)


def _back(x, qkv, h, w2, wo, dh):
    r, d = x.shape
    s, w = qkv.shape
    f = h.shape[1]
    hw = w // 3
    nh = hw // dh
    qb = 256
    c2 = dh ** -0.5 * 1.4426950408889634
    nblk = s // qb
    nt = 512
    cw = 256
    ck = 4096
    nk = f // ck
    nn = d // nt
    ring = 4
    ta, tw, to = nh, nn * nk // 2, nn // 2
    steps = ta + tw + to
    ntile2 = nn * nk
    ntiles = ntile2 + nn

    def body(x_ref, q_ref, k_ref, v_ref, h_ref, w2_ref, wo_ref, y_ref,
             kt, vx, pb, o_scr, o_send, o_all, h_scr, w_scr, acc, hsem, wsem, send, recv):
        step = pl.program_id(0)
        me = lax.axis_index("seq")
        near = me + 1 - 2 * (me % 2)
        members = [me, near, (me + 2) % 4, 3 - me]

        def load(i):
            slot = i % ring

            @pl.when(i < ntile2)
            def _():
                rows = pl.ds(pl.multiple_of((i % nk) * ck, ck), ck)
                cols = pl.ds(pl.multiple_of((i // nk) * nt, nt), nt)
                pltpu.make_async_copy(w2_ref.at[rows, cols], w_scr.at[slot], wsem.at[slot]).start()

            @pl.when((i >= ntile2) & (i < ntiles))
            def _():
                cols = pl.ds(pl.multiple_of((i - ntile2) * nt, nt), nt)
                pltpu.make_async_copy(wo_ref.at[:, cols], w_scr.at[slot], wsem.at[slot]).start()

        def ready(i):
            slot = i % ring
            pltpu.make_async_copy(wo_ref.at[:, pl.ds(0, nt)], w_scr.at[slot], wsem.at[slot]).wait()
            return slot

        def hcopy(c):
            return pltpu.make_async_copy(h_ref.at[:, pl.ds(c * ck, ck)], h_scr.at[c], hsem.at[c])

        def share(k):
            return pltpu.make_async_remote_copy(
                src_ref=o_send.at[k - 1],
                dst_ref=o_all.at[:, pl.ds(pl.multiple_of(me * hw, hw), hw)],
                send_sem=send.at[k - 1], recv_sem=recv.at[k - 1],
                device_id={"seq": members[k]}, device_id_type=MESH)

        for c in range(nk):
            @pl.when(step == c)
            def _(c=c):
                hcopy(c).start()

        for i in range(ring):
            @pl.when(step == ta - ring + i)
            def _(i=i):
                load(i)

        bar = pltpu.get_barrier_semaphore()

        @pl.when(step == 0)
        def _():
            for k in range(1, 4):
                pl.semaphore_signal(bar, inc=1, device_id={"seq": members[k]}, device_id_type=MESH)
            vx[:, dh:] = jnp.ones((s, dh), BF16)

        row = lax.broadcasted_iota(jnp.int32, (qb, qb), 0)
        col = lax.broadcasted_iota(jnp.int32, (qb, qb), 1)
        keep = col <= row

        def scores(b):
            q = q_ref[b * qb:(b + 1) * qb, :]
            m = None
            for c in range(b + 1):
                cols = slice(c * qb, (c + 1) * qb)
                t = _dot(q, kt[:, cols])
                if c == b:
                    t = jnp.where(keep, t, NEG)
                acc[(b % 2) * (s // nt) + c * qb // nt, :qb, (c * qb) % nt:(c * qb) % nt + qb] = t
                for g in range(qb // dh):
                    u = t[:, g * dh:(g + 1) * dh]
                    m = u if m is None else jnp.maximum(m, u)
            return jnp.max(m, axis=-1, keepdims=True) * c2

        def finish(b, m):
            n = (b + 1) * qb
            for c in range(b + 1):
                t = acc[(b % 2) * (s // nt) + c * qb // nt, :qb, (c * qb) % nt:(c * qb) % nt + qb]
                pb[b % 2, :, c * qb:(c + 1) * qb] = jnp.exp2(t * c2 - m).astype(BF16)
            o = _dot(pb[b % 2, :, :n], vx[:n, :])
            o_scr[b * qb:n, :] = (o[:, :dh] / o[:, dh:]).astype(BF16)

        @pl.when(step < ta)
        def _():
            for c in range(nblk):
                cols = slice(c * qb, (c + 1) * qb)
                vx[cols, :dh] = v_ref[cols, :]
                kt[:, cols] = k_ref[cols, :].T
            m = scores(0)
            for b in range(nblk):
                ahead = scores(b + 1) if b + 1 < nblk else None
                finish(b, m)
                m = ahead
            own = pl.ds(pl.multiple_of(me * r, r), r)
            lanes = pl.ds(pl.multiple_of(step * dh, dh), dh)
            o_all[:, pl.ds(pl.multiple_of(me * hw + step * dh, dh), dh)] = o_scr[own, :]
            for k in range(1, 4):
                o_send[k - 1, :, lanes] = o_scr[pl.ds(pl.multiple_of(members[k] * r, r), r), :]

        @pl.when(step == ta)
        def _():
            pl.semaphore_wait(bar, 3)
            for k in (2, 3, 1):
                share(k).start()
            for c in range(nk // 2):
                hcopy(c).wait()

        @pl.when(step == ta + 1)
        def _():
            for c in range(nk // 2, nk):
                hcopy(c).wait()

        u = step - ta

        def second(first):
            slots = [ready(2 * u), ready(2 * u + 1)]
            kc = 2 * (u % 2)
            for c in range(nt // cw):
                cols = slice(c * cw, (c + 1) * cw)
                t = _dot(h_scr[kc], w_scr[slots[0], :, cols]) + _dot(h_scr[kc + 1], w_scr[slots[1], :, cols])
                acc[u // 2, :, cols] = t if first else acc[u // 2, :, cols] + t
            load(2 * u + ring)
            load(2 * u + ring + 1)

        pl.when((u >= 0) & (u < tw) & (u % 2 == 0))(lambda: second(True))
        pl.when((u >= 0) & (u < tw) & (u % 2 == 1))(lambda: second(False))

        @pl.when(u == tw)
        def _():
            for k in range(1, 4):
                share(k).wait_recv()

        @pl.when(u >= tw)
        def _():
            slots = [ready(2 * u), ready(2 * u + 1)]
            for half, slot in enumerate(slots):
                for c in range(nt // cw):
                    cols = slice(c * cw, (c + 1) * cw)
                    out = slice(half * nt + c * cw, half * nt + (c + 1) * cw)
                    t = _dot(o_all[...], w_scr[slot, :, cols])
                    t = (x_ref[:, out].astype(F32) + t) + acc[2 * (u - tw) + half, :, cols]
                    y_ref[:, out] = t.astype(BF16)
            load(2 * u + ring)
            load(2 * u + ring + 1)

        @pl.when(step == steps - 1)
        def _():
            for k in range(1, 4):
                share(k).wait_send()

    def col(base):
        return pl.BlockSpec((s, dh), lambda i: (0, base + jnp.minimum(i, nh - 1)))

    tile = pl.BlockSpec((r, 2 * nt), lambda i: (0, jnp.clip(i - ta - tw, 0, to - 1)))
    anyspace = pl.BlockSpec(memory_space=pl.ANY)
    return pl.pallas_call(
        body,
        grid=(steps,),
        in_specs=[tile, col(0), col(nh), col(2 * nh)] + [anyspace] * 3,
        out_specs=tile,
        out_shape=jax.ShapeDtypeStruct((r, d), BF16),
        scratch_shapes=[
            pltpu.VMEM((dh, s), BF16), pltpu.VMEM((s, 2 * dh), BF16), pltpu.VMEM((2, qb, s), BF16),
            pltpu.VMEM((s, dh), BF16), pltpu.VMEM((3, r, hw), BF16), pltpu.VMEM((r, 4 * hw), BF16),
            pltpu.VMEM((nk, r, ck), BF16), pltpu.VMEM((ring, ck, nt), BF16), pltpu.VMEM((nn, r, nt), F32),
            pltpu.SemaphoreType.DMA((nk,)), pltpu.SemaphoreType.DMA((ring,)),
            pltpu.SemaphoreType.DMA((3,)), pltpu.SemaphoreType.DMA((3,))],
        compiler_params=pltpu.CompilerParams(
            dimension_semantics=("arbitrary",), vmem_limit_bytes=63 * 1024 * 1024, collective_id=1,
            has_side_effects=True),
        name="back",
        cost_estimate=_cost(4 * s * s * dh * nh + 2 * r * d * (f + 4 * hw), 2 * d * (f + 4 * hw)),
    )(x, qkv, qkv, qkv, h, w2, wo)


def solution(mesh):
    nseq = mesh.shape["seq"]

    def local(x, g1, b1, g2, b2, wqkv, wo, w1, w2):
        nh, dh, d = wo.shape
        r = x.shape[0]
        h, qkv = _front(x, g1, b1, g2, b2, _rope_tables(nseq * r, dh), wqkv, w1)
        return _back(x, qkv, h, w2, wo.reshape(nh * dh, d), dh)

    rows = P(("data", "seq"), None)
    rep = P()
    return jax.shard_map(local, mesh=mesh,
                         in_specs=(rows, rep, rep, rep, rep, rep, rep, rep, rep),
                         out_specs=rows, check_vma=False)
```

profile of v0, /device:TPU:11, one launch (start us, length us, event | category | flops | bytes accessed | tf_op | source)
XLA Modules:
  0.0 273.9 jit_solution(3033163514240226444)
XLA Ops:
  0.0 0.8 multiply_sine_fusion.1
  0.8 0.8 multiply_sine_fusion
  1.6 144.5 %front.1 = (bf16[512,16384]{1,0:T(8,128)(2,1)}, bf16[2048,3072]{1,0:T(8,128)(2,1)}) custom-call(bf16[512,4096]{1,0:T(8,128)(2,1)} %x_ref.3, f32[1,4096]{1,0:T(1,128)} %bitcast.6, f32[1,4096]{1,0:T(1,128)} %bitcast.7, f32[1,4096]{1,0:T(1,128)} %bitcast.8, f32[1,4096]{1,0:T(1,128)} %bitcast.9, f32[64,128]{1,0:T(8,128)} %get-tuple-element.12.cl, ...), custom_call_target="tpu_custom_call" | custom-call | flops 120259084288 | bytes 184549376 | tf_op jit(solution)/shard_map/front/pallas_call | solution.py:250
  146.1 123.1 %back.1 = bf16[512,4096]{1,0:T(8,128)(2,1)} custom-call(bf16[512,4096]{1,0:T(8,128)(2,1)} %x_ref.3, bf16[2048,3072]{1,0:T(8,128)(2,1)} %get-tuple-element.7.q_ref.k_ref.v_ref, bf16[2048,3072]{1,0:T(8,128)(2,1)} %get-tuple-element.7.q_ref.k_ref.v_ref, bf16[2048,3072]{1,0:T(8,128)(2,1)} %get-tuple-element.7.q_ref.k_ref.v_ref, ...), custom_call_target="tpu_custom_call" | custom-call | flops 103079215104 | bytes 167772160 | tf_op jit(solution)/shard_map/back/pallas_call | solution.py:442
  269.2 4.7 %copy.11 = bf16[512,4096]{1,0:T(8,128)(2,1)} copy(bf16[512,4096]{1,0:T(8,128)(2,1)} %back.1) | data formatting | bytes 8388608
  (3 shorter events, 0.0 us)
where the time goes:
time: 274 us
  Pallas kernels  268 us (98%)
  local copies, waits for them, and re-layouts  4.7 us (2%)
    pallas_call x1, Pallas kernels, _front(): pl.pallas_call(body, grid=(steps,), in_specs=[anyspace] + [full((1, d))]...  145 us
    pallas_call x1, Pallas kernels, _back(): pl.pallas_call(body, grid=(steps,), in_specs=[tile, col(0), col(nh), col(...  123 us

commit v1 on v0

v1 whole, which is shorter than its diff:
```python
import functools

import jax
import jax.numpy as jnp
from jax import lax
from jax.experimental import pallas as pl
from jax.experimental.pallas import tpu as pltpu
from jax.sharding import PartitionSpec as P

EPS = 1e-5
NEG = -1e30
F32 = jnp.float32
BF16 = jnp.bfloat16
VMEM = 60 * 1024 * 1024


def _cost(flops, nbytes):
    return pl.CostEstimate(flops=int(flops), bytes_accessed=int(nbytes), transcendentals=0)


def _dot(a, b):
    return jnp.dot(a, b, preferred_element_type=F32)


MESH = pl.DeviceIdType.MESH
LO = 64


def _rope_angles(s, dh):
    half = dh // 2
    e = lax.broadcasted_iota(jnp.int32, (1, dh), 1)
    inv = 10000.0 ** (-2.0 * (e % half).astype(F32) / dh)
    lo = jnp.arange(LO).astype(F32)[:, None] * inv
    hi = (LO * jnp.arange(s // LO)).astype(F32)[:, None] * inv
    return lo, hi


def _front(x, g1, b1, g2, b2, angles, wqkv, w1):
    r, d = x.shape
    f = w1.shape[1]
    w3 = wqkv.shape[1] // 3
    hw = w3 // 4
    dh = angles[0].shape[1]
    nt = 512
    mt = 2 * nt
    cw = 256
    t1 = f // mt
    nb = hw // nt
    t2 = 3 * nb
    ntile1 = f // nt
    ring = 5
    xc = 128

    def body(x_ref, g1_ref, b1_ref, g2_ref, b2_ref, lo_ref, hi_ref, wqkv_ref, w1_ref,
             h_ref, qkv_ref, x_scr, rows, m_scr, w_scr, t_scr, cos_s, sin_s, h_buf, q_buf,
             xsem, wsem, hsem, qsem, send, recv):
        me = lax.axis_index("seq")
        core = me % 2
        near = me + 1 - 2 * core
        far = (me + 2) % 4

        def member(k):
            return [me, near, far, 3 - me][k]

        def load1(i):
            c = pl.multiple_of(i * nt, nt)
            pltpu.make_async_copy(w1_ref.at[:, pl.ds(c, nt)], w_scr.at[i % ring], wsem.at[i % ring]).start()

        def load2(i):
            slot = (i + ntile1) % ring
            v = i % t2
            c = pl.multiple_of((v // nb) * w3 + me * hw + (v % nb) * nt, nt)
            pltpu.make_async_copy(wqkv_ref.at[:, pl.ds(c, nt)], w_scr.at[slot], wsem.at[slot]).start()

        def ready(i):
            slot = i % ring
            pltpu.make_async_copy(w1_ref.at[:, pl.ds(0, nt)], w_scr.at[slot], wsem.at[slot]).wait()
            return slot

        def remote(src, dst, part, sem, dev):
            return pltpu.make_async_remote_copy(
                src_ref=rows.at[src, part], dst_ref=rows.at[dst, part], send_sem=send.at[sem],
                recv_sem=recv.at[sem], device_id={"seq": dev}, device_id_type=MESH)

        def to_near():
            return remote(0, 1, pl.ds(0, r), 0, near)

        def to_far(p):
            return remote(0, 2, pl.ds(p * (r // 2), r // 2), 1 + p, far)

        def onward(p):
            return remote(2, 3, pl.ds(p * (r // 2), r // 2), 3 + p, near)

        def norm(c, q, _):
            base = c * xc + q * 32
            groups = [pl.ds(pl.multiple_of(base + 16 * g, 16), 16) for g in range(2)]
            nl = d // 128

            def col(rs, j):
                return x_scr[rs, j * 128:(j + 1) * 128].astype(F32)

            def total(f):
                part = [[None] * 4 for _ in groups]
                for j in range(nl):
                    for g, rs in enumerate(groups):
                        v = f(g, col(rs, j))
                        part[g][j % 4] = v if part[g][j % 4] is None else part[g][j % 4] + v
                return [jnp.sum((p[0] + p[1]) + (p[2] + p[3]), axis=-1, keepdims=True) / d for p in part]

            mu = total(lambda g, v: v)
            var = total(lambda g, v: (v - mu[g]) * (v - mu[g]))
            rs_ = [lax.rsqrt(v + EPS) for v in var]
            for j in range(nl):
                cs = slice(j * 128, (j + 1) * 128)
                for g, rs in enumerate(groups):
                    xn = (col(rs, j) - mu[g]) * rs_[g]
                    rows[0, rs, cs] = (xn * g1_ref[:, cs] + b1_ref[:, cs]).astype(BF16)
                    m_scr[rs, cs] = (xn * g2_ref[:, cs] + b2_ref[:, cs]).astype(BF16)
            return 0

        def chunk(c):
            rs = pl.ds(c * xc, xc)
            return pltpu.make_async_copy(x_ref.at[rs], x_scr.at[rs], xsem.at[c])

        for c in range(r // xc):
            chunk(c).start()
        for i in range(ring):
            load1(i)
        bar = pltpu.get_barrier_semaphore()
        for dev in (near, far):
            pl.semaphore_signal(bar, inc=1, device_id={"seq": dev}, device_id_type=MESH)
        neg = lax.broadcasted_iota(jnp.int32, (LO, dh), 1) < dh // 2
        cl, sl = jnp.cos(lo_ref[...]), jnp.sin(lo_ref[...])
        cos_s[0, :hi_ref.shape[0], :] = jnp.cos(hi_ref[...])
        sin_s[0, :hi_ref.shape[0], :] = jnp.sin(hi_ref[...])
        n = r // LO
        highs = []
        for k in range(4):
            base = pl.ds(pl.multiple_of(member(k) * n, n), n)
            highs.append((cos_s[0, base, :], sin_s[0, base, :]))
        for k, (hc, hs) in enumerate(highs):
            for i in range(n):
                a, b = hc[i:i + 1], hs[i:i + 1]
                sn = b * cl + a * sl
                cos_s[k, i * LO:(i + 1) * LO, :] = a * cl - b * sl
                sin_s[k, i * LO:(i + 1) * LO, :] = jnp.where(neg, -sn, sn)
        for c in range(r // xc):
            chunk(c).wait()
            lax.fori_loop(0, xc // 32, functools.partial(norm, c), 0)
            if c == r // xc // 2 - 1:
                pl.semaphore_wait(bar, 2)
                to_far(0).start()
        to_far(1).start()
        to_near().start()

        def h_out(i):
            c = pl.multiple_of(i * mt, mt)
            return pltpu.make_async_copy(h_buf.at[i % 2], h_ref.at[:, pl.ds(c, mt)], hsem.at[i % 2])

        def q_out(i):
            v = i % t2
            chip = me // 2
            pair = chip + (i // t2) * (1 - 2 * chip)
            rs = pl.ds(pl.multiple_of(pair * 2 * r, 2 * r), 2 * r)
            c = pl.multiple_of(v * nt, nt)
            return pltpu.make_async_copy(q_buf.at[i % 2], qkv_ref.at[rs, pl.ds(c, nt)], qsem.at[i % 2])


        def gelu(i, cols):
            t = t_scr[:, cols]
            h_buf[i % 2, :, cols] = (0.5 * t * (1.0 + lax.erf(t * (0.5 ** 0.5)))).astype(BF16)

        def mlp(s, first):
            slots = [ready(2 * s + half) for half in range(mt // nt)]
            for half, slot in enumerate(slots):
                for c in range(nt // cw):
                    cols = slice(half * nt + c * cw, half * nt + (c + 1) * cw)
                    if not first:
                        gelu(s - 1, cols)
                    t_scr[:, cols] = _dot(m_scr[...], w_scr[slot, :, c * cw:(c + 1) * cw])
            if not first:
                h_out(s - 1).start()

        def rope(i, j):
            isv = (i % t2) // nb == 2
            base = 2 * (i // t2)
            k, c = j // (nt // cw), j % (nt // cw)
            out = pl.ds(pl.multiple_of((core if k == 0 else 1 - core) * r, r), r)
            t = t_scr[:, j * cw:(j + 1) * cw].astype(BF16).astype(F32)
            for hd in range(cw // dh):
                p = t[:, hd * dh:(hd + 1) * dh]
                v = p * cos_s[base + k] + pltpu.roll(p, dh // 2, 1) * sin_s[base + k]
                lo = c * cw + hd * dh
                q_buf[i % 2, out, lo:lo + dh] = jnp.where(isv, p, v).astype(BF16)

        def qkv(u, first):
            slot = ready(ntile1 + u)
            base = 2 * (u // t2)
            for j in range(mt // cw):
                cols = slice(j * cw, (j + 1) * cw)
                k, c = j // (nt // cw), j % (nt // cw)
                if first:
                    gelu(t1 - 1, cols)
                else:
                    rope(u - 1, j)
                t_scr[:, cols] = _dot(rows[base + k], w_scr[slot, :, c * cw:(c + 1) * cw])

        mlp(0, True)
        load1(ring)
        load1(ring + 1)

        inner = (ntile1 - ring - 2) // 2 + 1

        def mlp_step(s, _):
            @pl.when(s > 2)
            def _():
                h_out(s - 3).wait()

            mlp(s, False)

            @pl.when(s < inner)
            def _():
                load1(2 * s + ring)
                load1(2 * s + ring + 1)

            @pl.when(s >= inner)
            def _():
                i = 2 * s + ring

                @pl.when(i < ntile1)
                def _():
                    load1(i)

                @pl.when(i >= ntile1)
                def _():
                    load2(i - ntile1)

                load2(i + 1 - ntile1)
            return 0

        lax.fori_loop(1, t1, mlp_step, 0)

        to_near().wait_recv()
        to_far(0).wait_recv()
        onward(0).start()
        h_out(t1 - 3).wait()
        qkv(0, True)
        h_out(t1 - 1).start()
        load2(ring)

        def qkv_step(u, _):
            @pl.when(u == t2 - 2)
            def _():
                to_far(1).wait_recv()
                onward(1).start()

            @pl.when(u == t2)
            def _():
                onward(0).wait_recv()
                onward(1).wait_recv()

            @pl.when(u > 2)
            def _():
                q_out(u - 3).wait()

            qkv(u, False)
            q_out(u - 1).start()

            @pl.when(u + ring < 2 * t2)
            def _():
                load2(u + ring)
            return 0

        lax.fori_loop(1, 2 * t2, qkv_step, 0)
        q_out(2 * t2 - 3).wait()
        for j in range(mt // cw):
            rope(2 * t2 - 1, j)
        q_out(2 * t2 - 1).start()
        h_out(t1 - 2).wait()
        h_out(t1 - 1).wait()
        q_out(2 * t2 - 2).wait()
        q_out(2 * t2 - 1).wait()
        to_near().wait_send()
        for p in range(2):
            to_far(p).wait_send()
            onward(p).wait_send()

    anyspace = pl.BlockSpec(memory_space=pl.ANY)
    inside = pl.BlockSpec(memory_space=pltpu.VMEM)
    return pl.pallas_call(
        body,
        in_specs=[anyspace] + [inside] * 6 + [anyspace] * 2,
        out_specs=[anyspace, anyspace],
        out_shape=[jax.ShapeDtypeStruct((r, f), BF16), jax.ShapeDtypeStruct((4 * r, 3 * hw), BF16)],
        scratch_shapes=[
            pltpu.VMEM((r, d), BF16), pltpu.VMEM((4, r, d), BF16), pltpu.VMEM((r, d), BF16),
            pltpu.VMEM((ring, d, nt), BF16),
            pltpu.VMEM((r, mt), F32), pltpu.VMEM((4, r, dh), F32), pltpu.VMEM((4, r, dh), F32),
            pltpu.VMEM((2, r, mt), BF16), pltpu.VMEM((2, 2 * r, nt), BF16),
            pltpu.SemaphoreType.DMA((r // xc,)), pltpu.SemaphoreType.DMA((ring,)),
            pltpu.SemaphoreType.DMA((2,)), pltpu.SemaphoreType.DMA((2,)),
            pltpu.SemaphoreType.DMA((5,)), pltpu.SemaphoreType.DMA((5,))],
        compiler_params=pltpu.CompilerParams(
            vmem_limit_bytes=VMEM, collective_id=0, has_side_effects=True),
        name="front",
        cost_estimate=_cost(2 * r * d * f + 2 * 4 * r * d * 3 * hw, 2 * d * f + 4 * d * 3 * hw),
    )(x, g1[None], b1[None], g2[None], b2[None], *angles, wqkv, w1)


def _back(x, qkv, h, w2, wo, dh):
    r, d = x.shape
    s, w = qkv.shape
    f = h.shape[1]
    hw = w // 3
    nh = hw // dh
    qb = 256
    c2 = dh ** -0.5 * 1.4426950408889634
    nblk = s // qb
    nt = 512
    cw = 256
    ck = 4096
    nk = f // ck
    nn = d // nt
    ring = 4
    to = nn // 2
    ntile2 = nn * nk

    def body(x_ref, qkv_ref, h_ref, w2_ref, wo_ref, y_ref,
             qkv_buf, kt, vx, pb, o_scr, o_send, o_all, h_scr, w_scr, acc, x_buf, y_buf,
             asem, hsem, wsem, xsem, ysem, send, recv):
        me = lax.axis_index("seq")
        near = me + 1 - 2 * (me % 2)
        members = [me, near, (me + 2) % 4, 3 - me]

        def load(i, wo=False):
            slot = i % ring
            if wo:
                src = wo_ref.at[:, pl.ds(pl.multiple_of((i - ntile2) * nt, nt), nt)]
            else:
                rows = pl.ds(pl.multiple_of((i % nk) * ck, ck), ck)
                src = w2_ref.at[rows, pl.ds(pl.multiple_of((i // nk) * nt, nt), nt)]
            pltpu.make_async_copy(src, w_scr.at[slot], wsem.at[slot]).start()

        def heads(i):
            return [pltpu.make_async_copy(
                qkv_ref.at[:, pl.ds(pl.multiple_of(t * hw + i * dh, dh), dh)],
                qkv_buf.at[i % 2, t], asem.at[i % 2, t]) for t in range(3)]

        def x_in(i):
            cols = pl.ds(pl.multiple_of(i * 2 * nt, 2 * nt), 2 * nt)
            return pltpu.make_async_copy(x_ref.at[:, cols], x_buf.at[i % 2], xsem.at[i % 2])

        def y_out(i):
            cols = pl.ds(pl.multiple_of(i * 2 * nt, 2 * nt), 2 * nt)
            return pltpu.make_async_copy(y_buf.at[i % 2], y_ref.at[:, cols], ysem.at[i % 2])

        def ready(i):
            slot = i % ring
            pltpu.make_async_copy(wo_ref.at[:, pl.ds(0, nt)], w_scr.at[slot], wsem.at[slot]).wait()
            return slot

        def hcopy(c):
            return pltpu.make_async_copy(h_ref.at[:, pl.ds(c * ck, ck)], h_scr.at[c], hsem.at[c])

        def share(k):
            return pltpu.make_async_remote_copy(
                src_ref=o_send.at[k - 1],
                dst_ref=o_all.at[:, pl.ds(pl.multiple_of(me * hw, hw), hw)],
                send_sem=send.at[k - 1], recv_sem=recv.at[k - 1],
                device_id={"seq": members[k]}, device_id_type=MESH)

        for t in heads(0):
            t.start()
        bar = pltpu.get_barrier_semaphore()
        for k in range(1, 4):
            pl.semaphore_signal(bar, inc=1, device_id={"seq": members[k]}, device_id_type=MESH)
        vx[:, dh:] = jnp.ones((s, dh), BF16)

        row = lax.broadcasted_iota(jnp.int32, (qb, qb), 0)
        col = lax.broadcasted_iota(jnp.int32, (qb, qb), 1)
        keep = col <= row

        def scores(i, b):
            q = qkv_buf[i % 2, 0, b * qb:(b + 1) * qb, :]
            m = None
            for c in range(b + 1):
                cols = slice(c * qb, (c + 1) * qb)
                t = _dot(q, kt[:, cols])
                if c == b:
                    t = jnp.where(keep, t, NEG)
                acc[(b % 2) * (s // nt) + c * qb // nt, :qb, (c * qb) % nt:(c * qb) % nt + qb] = t
                for g in range(qb // dh):
                    u = t[:, g * dh:(g + 1) * dh]
                    m = u if m is None else jnp.maximum(m, u)
            return jnp.max(m, axis=-1, keepdims=True) * c2

        def finish(b, m):
            n = (b + 1) * qb
            for c in range(b + 1):
                t = acc[(b % 2) * (s // nt) + c * qb // nt, :qb, (c * qb) % nt:(c * qb) % nt + qb]
                pb[b % 2, :, c * qb:(c + 1) * qb] = jnp.exp2(t * c2 - m).astype(BF16)
            o = _dot(pb[b % 2, :, :n], vx[:n, :])
            o_scr[b * qb:n, :] = (o[:, :dh] / o[:, dh:]).astype(BF16)

        def head(i, _):
            @pl.when(i + 1 < nh)
            def _():
                for t in heads(i + 1):
                    t.start()

            for c in range(nk):
                @pl.when(i == c)
                def _(c=c):
                    hcopy(c).start()

            for c in range(ring):
                @pl.when(i == nh - ring + c)
                def _(c=c):
                    load(c)

            for t in heads(i):
                t.wait()
            for c in range(nblk):
                cols = slice(c * qb, (c + 1) * qb)
                vx[cols, :dh] = qkv_buf[i % 2, 2, cols, :]
                kt[:, cols] = qkv_buf[i % 2, 1, cols, :].T
            m = scores(i, 0)
            for b in range(nblk):
                ahead = scores(i, b + 1) if b + 1 < nblk else None
                finish(b, m)
                m = ahead
            own = pl.ds(pl.multiple_of(me * r, r), r)
            lanes = pl.ds(pl.multiple_of(i * dh, dh), dh)
            o_all[:, pl.ds(pl.multiple_of(me * hw + i * dh, dh), dh)] = o_scr[own, :]
            for k in range(1, 4):
                o_send[k - 1, :, lanes] = o_scr[pl.ds(pl.multiple_of(members[k] * r, r), r), :]
            return 0

        lax.fori_loop(0, nh, head, 0)
        pl.semaphore_wait(bar, 3)
        for k in (2, 3, 1):
            share(k).start()
        for c in range(nk):
            hcopy(c).wait()

        def second(n, half):
            slots = [ready(nk * n + 2 * half), ready(nk * n + 2 * half + 1)]
            kc = 2 * half
            for c in range(nt // cw):
                cols = slice(c * cw, (c + 1) * cw)
                t = _dot(h_scr[kc], w_scr[slots[0], :, cols]) + _dot(h_scr[kc + 1], w_scr[slots[1], :, cols])
                acc[n, :, cols] = acc[n, :, cols] + t if half else t

        def w2_step(n, _):
            for half in range(nk // 2):
                second(n, half)

                @pl.when(n < nn - 1)
                def _():
                    load(nk * (n + 1) + 2 * half)
                    load(nk * (n + 1) + 2 * half + 1)

                @pl.when(n == nn - 1)
                def _():
                    load(nk * nn + 2 * half, wo=True)
                    load(nk * nn + 2 * half + 1, wo=True)
            return 0

        x_in(0).start()
        lax.fori_loop(0, nn, w2_step, 0)
        for k in range(1, 4):
            share(k).wait_recv()

        def wo_step(n, _):
            @pl.when(n + 1 < to)
            def _():
                x_in(n + 1).start()

            x_in(n).wait()

            @pl.when(n > 1)
            def _():
                y_out(n - 2).wait()

            slots = [ready(ntile2 + 2 * n), ready(ntile2 + 2 * n + 1)]
            for half, slot in enumerate(slots):
                for c in range(nt // cw):
                    cols = slice(c * cw, (c + 1) * cw)
                    out = slice(half * nt + c * cw, half * nt + (c + 1) * cw)
                    t = _dot(o_all[...], w_scr[slot, :, cols])
                    t = (x_buf[n % 2, :, out].astype(F32) + t) + acc[2 * n + half, :, cols]
                    y_buf[n % 2, :, out] = t.astype(BF16)
            y_out(n).start()

            @pl.when(n + 2 < to)
            def _():
                load(ntile2 + 2 * n + ring, wo=True)
                load(ntile2 + 2 * n + ring + 1, wo=True)
            return 0

        lax.fori_loop(0, to, wo_step, 0)
        y_out(to - 2).wait()
        y_out(to - 1).wait()
        for k in range(1, 4):
            share(k).wait_send()

    anyspace = pl.BlockSpec(memory_space=pl.ANY)
    return pl.pallas_call(
        body,
        in_specs=[anyspace] * 5,
        out_specs=anyspace,
        out_shape=jax.ShapeDtypeStruct((r, d), BF16),
        scratch_shapes=[
            pltpu.VMEM((2, 3, s, dh), BF16),
            pltpu.VMEM((dh, s), BF16), pltpu.VMEM((s, 2 * dh), BF16), pltpu.VMEM((2, qb, s), BF16),
            pltpu.VMEM((s, dh), BF16), pltpu.VMEM((3, r, hw), BF16), pltpu.VMEM((r, 4 * hw), BF16),
            pltpu.VMEM((nk, r, ck), BF16), pltpu.VMEM((ring, ck, nt), BF16), pltpu.VMEM((nn, r, nt), F32),
            pltpu.VMEM((2, r, 2 * nt), BF16), pltpu.VMEM((2, r, 2 * nt), BF16),
            pltpu.SemaphoreType.DMA((2, 3)), pltpu.SemaphoreType.DMA((nk,)), pltpu.SemaphoreType.DMA((ring,)),
            pltpu.SemaphoreType.DMA((2,)), pltpu.SemaphoreType.DMA((2,)),
            pltpu.SemaphoreType.DMA((3,)), pltpu.SemaphoreType.DMA((3,))],
        compiler_params=pltpu.CompilerParams(
            vmem_limit_bytes=63 * 1024 * 1024, collective_id=1,
            has_side_effects=True),
        name="back",
        cost_estimate=_cost(4 * s * s * dh * nh + 2 * r * d * (f + 4 * hw), 2 * d * (f + 4 * hw)),
    )(x, qkv, h, w2, wo)


def solution(mesh):
    nseq = mesh.shape["seq"]

    def local(x, g1, b1, g2, b2, wqkv, wo, w1, w2):
        nh, dh, d = wo.shape
        r = x.shape[0]
        h, qkv = _front(x, g1, b1, g2, b2, _rope_angles(nseq * r, dh), wqkv, w1)
        return _back(x, qkv, h, w2, wo.reshape(nh * dh, d), dh)

    rows = P(("data", "seq"), None)
    rep = P()
    return jax.shard_map(local, mesh=mesh,
                         in_specs=(rows, rep, rep, rep, rep, rep, rep, rep, rep),
                         out_specs=rows, check_vma=False)
```

time: 274 us -> 264 us (0.964)
  Pallas kernels: 268 us -> 258 us
    pallas_call x2, Pallas kernels: 268 us -> 258 us  [the longest x1 140 us: _front(): pl.pallas_call(body, in_specs=[anyspace] + [inside] * 6 + [anyspace] * 2,...]
where the time goes in v1:
time: 264 us
  Pallas kernels  258 us (98%)
  local copies, waits for them, and re-layouts  4.7 us (2%)
    pallas_call x1, Pallas kernels, _front(): pl.pallas_call(body, in_specs=[anyspace] + [inside] * 6 + [anyspace] * 2,...  140 us
    pallas_call x1, Pallas kernels, _back(): pl.pallas_call(body, in_specs=[anyspace] * 5, out_specs=anyspace, out_sha...  118 us

profile of v1, /device:TPU:11, one launch (start us, length us, event | category | flops | bytes accessed | tf_op | source)
XLA Modules:
  0.0 264.1 jit_solution(10545202024868457541)
XLA Ops:
  0.0 0.7 broadcast_multiply_fusion.1.hi_ref
  0.7 0.7 broadcast_multiply_fusion.lo_ref
  1.4 140.0 %front.1 = (bf16[512,16384]{1,0:T(8,128)(2,1)}, bf16[2048,3072]{1,0:T(8,128)(2,1)}) custom-call(bf16[512,4096]{1,0:T(8,128)(2,1)} %x_ref.3, f32[1,4096]{1,0:T(1,128)} %bitcast.6, f32[1,4096]{1,0:T(1,128)} %bitcast.7, f32[1,4096]{1,0:T(1,128)} %bitcast.8, f32[1,4096]{1,0:T(1,128)} %bitcast.9, f32[64,128]{1,0:T(8,128)} %broadcast_multiply_fusion.lo_ref, ...), custom_call_target="tpu_custom_call" | custom-call | flops 120259084288 | bytes 184549376 | tf_op jit(solution)/shard_map/front/pallas_call | solution.py:290
  141.4 117.9 %back.1 = bf16[512,4096]{1,0:T(8,128)(2,1)} custom-call(bf16[512,4096]{1,0:T(8,128)(2,1)} %x_ref.3, bf16[2048,3072]{1,0:T(8,128)(2,1)} %get-tuple-element.7.qkv_ref, bf16[512,16384]{1,0:T(8,128)(2,1)} %get-tuple-element.8.h_ref, bf16[16384,4096]{1,0:T(8,128)(2,1)} %w2_ref.1, bf16[4096,4096]{1,0:T(8,128)(2,1)} %bitcast.5), custom_call_target="tpu_custom_call" | custom-call | flops 103079215104 | bytes 167772160 | tf_op jit(solution)/shard_map/back/pallas_call | solution.py:508
  259.4 4.7 %copy.11 = bf16[512,4096]{1,0:T(8,128)(2,1)} copy(bf16[512,4096]{1,0:T(8,128)(2,1)} %back.1) | data formatting | bytes 8388608
  (3 shorter events, 0.0 us)

commit v2 on v1

--- a/solution.py
+++ b/solution.py
@@ -2,6 +2,7 @@
 
 import jax
 import jax.numpy as jnp
+import numpy as np
 from jax import lax
 from jax.experimental import pallas as pl
 from jax.experimental.pallas import tpu as pltpu
@@ -26,21 +27,18 @@
 LO = 64
 
 
-def _rope_angles(s, dh):
-    half = dh // 2
-    e = lax.broadcasted_iota(jnp.int32, (1, dh), 1)
-    inv = 10000.0 ** (-2.0 * (e % half).astype(F32) / dh)
-    lo = jnp.arange(LO).astype(F32)[:, None] * inv
-    hi = (LO * jnp.arange(s // LO)).astype(F32)[:, None] * inv
-    return lo, hi
-
-
-def _front(x, g1, b1, g2, b2, angles, wqkv, w1):
+def _inverse_frequencies(dh):
+    e = np.arange(dh) % (dh // 2)
+    return np.asarray(10000.0 ** (-2.0 * e / dh), np.float32)[None]
+
+
+def _front(x, g1, b1, g2, b2, inv, wqkv, w1):
     r, d = x.shape
     f = w1.shape[1]
     w3 = wqkv.shape[1] // 3
     hw = w3 // 4
-    dh = angles[0].shape[1]
+    dh = inv.shape[1]
+    highs = 4 * r // LO
     nt = 512
     mt = 2 * nt
     cw = 256
@@ -51,7 +49,7 @@
     ring = 5
     xc = 128
 
-    def body(x_ref, g1_ref, b1_ref, g2_ref, b2_ref, lo_ref, hi_ref, wqkv_ref, w1_ref,
+    def body(x_ref, g1_ref, b1_ref, g2_ref, b2_ref, inv_ref, wqkv_ref, w1_ref,
              h_ref, qkv_ref, x_scr, rows, m_scr, w_scr, t_scr, cos_s, sin_s, h_buf, q_buf,
              xsem, wsem, hsem, qsem, send, recv):
         me = lax.axis_index("seq")
@@ -130,15 +128,17 @@
         for dev in (near, far):
             pl.semaphore_signal(bar, inc=1, device_id={"seq": dev}, device_id_type=MESH)
         neg = lax.broadcasted_iota(jnp.int32, (LO, dh), 1) < dh // 2
-        cl, sl = jnp.cos(lo_ref[...]), jnp.sin(lo_ref[...])
-        cos_s[0, :hi_ref.shape[0], :] = jnp.cos(hi_ref[...])
-        sin_s[0, :hi_ref.shape[0], :] = jnp.sin(hi_ref[...])
+        lo = lax.broadcasted_iota(jnp.int32, (LO, dh), 0).astype(F32) * inv_ref[...]
+        hi = (LO * lax.broadcasted_iota(jnp.int32, (highs, dh), 0)).astype(F32) * inv_ref[...]
+        cl, sl = jnp.cos(lo), jnp.sin(lo)
+        cos_s[0, :highs, :] = jnp.cos(hi)
+        sin_s[0, :highs, :] = jnp.sin(hi)
         n = r // LO
-        highs = []
+        tables = []
         for k in range(4):
             base = pl.ds(pl.multiple_of(member(k) * n, n), n)
-            highs.append((cos_s[0, base, :], sin_s[0, base, :]))
-        for k, (hc, hs) in enumerate(highs):
+            tables.append((cos_s[0, base, :], sin_s[0, base, :]))
+        for k, (hc, hs) in enumerate(tables):
             for i in range(n):
                 a, b = hc[i:i + 1], hs[i:i + 1]
                 sn = b * cl + a * sl
@@ -289,7 +289,7 @@
     inside = pl.BlockSpec(memory_space=pltpu.VMEM)
     return pl.pallas_call(
         body,
-        in_specs=[anyspace] + [inside] * 6 + [anyspace] * 2,
+        in_specs=[anyspace] + [inside] * 5 + [anyspace] * 2,
         out_specs=[anyspace, anyspace],
         out_shape=[jax.ShapeDtypeStruct((r, f), BF16), jax.ShapeDtypeStruct((4 * r, 3 * hw), BF16)],
         scratch_shapes=[
@@ -304,7 +304,7 @@
             vmem_limit_bytes=VMEM, collective_id=0, has_side_effects=True),
         name="front",
         cost_estimate=_cost(2 * r * d * f + 2 * 4 * r * d * 3 * hw, 2 * d * f + 4 * d * 3 * hw),
-    )(x, g1[None], b1[None], g2[None], b2[None], *angles, wqkv, w1)
+    )(x, g1[None], b1[None], g2[None], b2[None], inv, wqkv, w1)
 
 
 def _back(x, qkv, h, w2, wo, dh):
@@ -527,14 +527,47 @@
     )(x, qkv, h, w2, wo)
 
 
+def _pass_on(y):
+    r, d = y.shape
+    n = 8
+    w = r // n
+
+    def body(y_ref, o_ref, buf, isem, osem):
+        def get(i):
+            rs = pl.ds(i * w, w)
+            return pltpu.make_async_copy(y_ref.at[rs], buf.at[i], isem.at[i])
+
+        def put(i):
+            rs = pl.ds(i * w, w)
+            return pltpu.make_async_copy(buf.at[i], o_ref.at[rs], osem.at[i])
+
+        for i in range(n):
+            get(i).start()
+        for i in range(n):
+            get(i).wait()
+            put(i).start()
+        for i in range(n):
+            put(i).wait()
+
+    anyspace = pl.BlockSpec(memory_space=pl.ANY)
+    return pl.pallas_call(
+        body, in_specs=[anyspace], out_specs=anyspace,
+        out_shape=jax.ShapeDtypeStruct((r, d), y.dtype),
+        scratch_shapes=[pltpu.VMEM((n, w, d), y.dtype), pltpu.SemaphoreType.DMA((n,)),
+                        pltpu.SemaphoreType.DMA((n,))],
+        compiler_params=pltpu.CompilerParams(vmem_limit_bytes=VMEM), name="pass_on",
+        cost_estimate=_cost(0, 4 * r * d),
+    )(y)
+
+
 def solution(mesh):
     nseq = mesh.shape["seq"]
 
     def local(x, g1, b1, g2, b2, wqkv, wo, w1, w2):
         nh, dh, d = wo.shape
         r = x.shape[0]
-        h, qkv = _front(x, g1, b1, g2, b2, _rope_angles(nseq * r, dh), wqkv, w1)
-        return _back(x, qkv, h, w2, wo.reshape(nh * dh, d), dh)
+        h, qkv = _front(x, g1, b1, g2, b2, jnp.asarray(_inverse_frequencies(dh)), wqkv, w1)
+        return _pass_on(_back(x, qkv, h, w2, wo.reshape(nh * dh, d), dh))
 
     rows = P(("data", "seq"), None)
     rep = P()

time: 264 us -> 262 us (level)
  local copies, waits for them, and re-layouts: 4.7 us -> 0 us
  Pallas kernels: 258 us -> 261 us
    unnamed x1 -> x0, local copies, waits for them, and re-layouts: 4.7 us -> none
    pallas_call x1 -> x2, Pallas kernels: 140 us -> 143 us  [the longest x1 140 us: _front(): pl.pallas_call(body, in_specs=[anyspace] + [inside] * 5 + [anyspace] * 2,...]
where the time goes in v2:
time: 262 us
  Pallas kernels  261 us (100%)
    pallas_call x1, Pallas kernels, _front(): pl.pallas_call(body, in_specs=[anyspace] + [inside] * 5 + [anyspace] * 2,...  140 us
    pallas_call x1, Pallas kernels, _back(): pl.pallas_call(body, in_specs=[anyspace] * 5, out_specs=anyspace, out_sha...  118 us

profile of v2, /device:TPU:11, one launch (start us, length us, event | category | flops | bytes accessed | tf_op | source)
XLA Modules:
  0.0 261.6 jit_solution(8602873572251192697)
XLA Ops:
  0.0 139.9 %front.1 = (bf16[512,16384]{1,0:T(8,128)(2,1)}, bf16[2048,3072]{1,0:T(8,128)(2,1)}) custom-call(bf16[512,4096]{1,0:T(8,128)(2,1)} %x_ref.3, f32[1,4096]{1,0:T(1,128)} %bitcast.6, f32[1,4096]{1,0:T(1,128)} %bitcast.7, f32[1,4096]{1,0:T(1,128)} %bitcast.8, f32[1,4096]{1,0:T(1,128)} %bitcast.9, f32[1,128]{1,0:T(1,128)} %constant.2.clone.inv_ref, ...), custom_call_target="tpu_custom_call" | custom-call | flops 120259084288 | bytes 184549376 | tf_op jit(solution)/shard_map/front/pallas_call | solution.py:290
  139.9 117.9 %back.1.y_ref = bf16[512,4096]{1,0:T(8,128)(2,1)} custom-call(bf16[512,4096]{1,0:T(8,128)(2,1)} %x_ref.3, bf16[2048,3072]{1,0:T(8,128)(2,1)} %get-tuple-element.7.qkv_ref, bf16[512,16384]{1,0:T(8,128)(2,1)} %get-tuple-element.8.h_ref, bf16[16384,4096]{1,0:T(8,128)(2,1)} %w2_ref.1, bf16[4096,4096]{1,0:T(8,128)(2,1)} %bitcast.5), custom_call_target="tpu_custom_call" | custom-call | flops 103079215104 | bytes 167772160 | tf_op jit(solution)/shard_map/back/pallas_call | solution.py:508
  257.8 3.6 %pass_on.1 = bf16[512,4096]{1,0:T(8,128)(2,1)} custom-call(bf16[512,4096]{1,0:T(8,128)(2,1)} %back.1.y_ref), custom_call_target="tpu_custom_call" | custom-call | bytes 8388608 | tf_op jit(solution)/shard_map/pass_on/pallas_call | solution.py:553

commit v3 on v2

--- a/solution.py
+++ b/solution.py
@@ -380,7 +380,7 @@
         col = lax.broadcasted_iota(jnp.int32, (qb, qb), 1)
         keep = col <= row
 
-        def scores(i, b):
+        def scores(i, b, w):
             q = qkv_buf[i % 2, 0, b * qb:(b + 1) * qb, :]
             m = None
             for c in range(b + 1):
@@ -388,18 +388,18 @@
                 t = _dot(q, kt[:, cols])
                 if c == b:
                     t = jnp.where(keep, t, NEG)
-                acc[(b % 2) * (s // nt) + c * qb // nt, :qb, (c * qb) % nt:(c * qb) % nt + qb] = t
+                acc[w * (s // nt) + c * qb // nt, :qb, (c * qb) % nt:(c * qb) % nt + qb] = t
                 for g in range(qb // dh):
                     u = t[:, g * dh:(g + 1) * dh]
                     m = u if m is None else jnp.maximum(m, u)
             return jnp.max(m, axis=-1, keepdims=True) * c2
 
-        def finish(b, m):
+        def finish(b, m, w):
             n = (b + 1) * qb
             for c in range(b + 1):
-                t = acc[(b % 2) * (s // nt) + c * qb // nt, :qb, (c * qb) % nt:(c * qb) % nt + qb]
-                pb[b % 2, :, c * qb:(c + 1) * qb] = jnp.exp2(t * c2 - m).astype(BF16)
-            o = _dot(pb[b % 2, :, :n], vx[:n, :])
+                t = acc[w * (s // nt) + c * qb // nt, :qb, (c * qb) % nt:(c * qb) % nt + qb]
+                pb[w, :, c * qb:(c + 1) * qb] = jnp.exp2(t * c2 - m).astype(BF16)
+            o = _dot(pb[w, :, :n], vx[:n, :])
             o_scr[b * qb:n, :] = (o[:, :dh] / o[:, dh:]).astype(BF16)
 
         def head(i, _):
@@ -424,10 +424,11 @@
                 cols = slice(c * qb, (c + 1) * qb)
                 vx[cols, :dh] = qkv_buf[i % 2, 2, cols, :]
                 kt[:, cols] = qkv_buf[i % 2, 1, cols, :].T
-            m = scores(i, 0)
-            for b in range(nblk):
-                ahead = scores(i, b + 1) if b + 1 < nblk else None
-                finish(b, m)
+            order = [nblk // 2 - 1] + [b for b in range(nblk)[::-1] if b != nblk // 2 - 1]
+            m = scores(i, order[0], 0)
+            for j, b in enumerate(order):
+                ahead = scores(i, order[j + 1], (j + 1) % 2) if j + 1 < nblk else None
+                finish(b, m, j % 2)
                 m = ahead
             own = pl.ds(pl.multiple_of(me * r, r), r)
             lanes = pl.ds(pl.multiple_of(i * dh, dh), dh)

time: 262 us -> 262 us (level)
  no operation moved by 1% of the time
where the time goes in v3:
time: 262 us; the launch traced here: 261 us
  Pallas kernels  261 us (100%)
    pallas_call x1, Pallas kernels, _front(): pl.pallas_call(body, in_specs=[anyspace] + [inside] * 5 + [anyspace] * 2,...  140 us
    pallas_call x1, Pallas kernels, _back(): pl.pallas_call(body, in_specs=[anyspace] * 5, out_specs=anyspace, out_sha...  118 us

profile of v3, /device:TPU:11, one launch (start us, length us, event | category | flops | bytes accessed | tf_op | source)
XLA Modules:
  0.0 261.4 jit_solution(6411885202121763698)
XLA Ops:
  0.0 139.9 %front.1 = (bf16[512,16384]{1,0:T(8,128)(2,1)}, bf16[2048,3072]{1,0:T(8,128)(2,1)}) custom-call(bf16[512,4096]{1,0:T(8,128)(2,1)} %x_ref.3, f32[1,4096]{1,0:T(1,128)} %bitcast.6, f32[1,4096]{1,0:T(1,128)} %bitcast.7, f32[1,4096]{1,0:T(1,128)} %bitcast.8, f32[1,4096]{1,0:T(1,128)} %bitcast.9, f32[1,128]{1,0:T(1,128)} %constant.2.clone.inv_ref, ...), custom_call_target="tpu_custom_call" | custom-call | flops 120259084288 | bytes 184549376 | tf_op jit(solution)/shard_map/front/pallas_call | solution.py:290
  139.9 117.8 %back.1.y_ref = bf16[512,4096]{1,0:T(8,128)(2,1)} custom-call(bf16[512,4096]{1,0:T(8,128)(2,1)} %x_ref.3, bf16[2048,3072]{1,0:T(8,128)(2,1)} %get-tuple-element.7.qkv_ref, bf16[512,16384]{1,0:T(8,128)(2,1)} %get-tuple-element.8.h_ref, bf16[16384,4096]{1,0:T(8,128)(2,1)} %w2_ref.1, bf16[4096,4096]{1,0:T(8,128)(2,1)} %bitcast.5), custom_call_target="tpu_custom_call" | custom-call | flops 103079215104 | bytes 167772160 | tf_op jit(solution)/shard_map/back/pallas_call | solution.py:509
  257.6 3.6 %pass_on.1 = bf16[512,4096]{1,0:T(8,128)(2,1)} custom-call(bf16[512,4096]{1,0:T(8,128)(2,1)} %back.1.y_ref), custom_call_target="tpu_custom_call" | custom-call | bytes 8388608 | tf_op jit(solution)/shard_map/pass_on/pallas_call | solution.py:554
